TPU v7x, 32 devices: a whole 2x2x4 slice. The times are simulated.
32 devices in a mesh: strip: 32 (over z, y, x, core).
Axes of the slice: x: 2, y: 2, z: 4, core: 2. Of those that a mesh axis runs over, the one named last changes fastest.
Arguments:
- state: float32 [4096, 4096], P('strip'), may hold values from -6 to 6
- noise: float32 [4096, 4096], P('strip'), may hold values from -6 to 6
- step: float32 [1], replicated, may hold values from 0.3 to 0.7
- field_scale: float32 [1], replicated, may hold values from 0.6 to 1.2
- wave_scale: float32 [1], replicated, may hold values from 4 to 8
- source: float32 [2048, 2048], P('strip'), may hold values from -6 to 6
- obs_cells: int32 [2048], replicated, may hold values from 0 to 4194303
- obs_values: float32 [2048], replicated, may hold values from -3 to 3
Outputs:
- log_perm: float32 [2048, 2048], P('strip')
- pressure: float32 [2048, 2048], P('strip')
- loglik: float32 [], replicated
Inputs may be any that keep to these rules, and one draw needn't show every extreme that they name: `obs_cells`: each entry is row * 2048 + column of an observed cell of the field grid.
All inputs are finite; a program needn't handle non-finite values.
Results may differ from a plain program's by a relative error of at most 0.00011.
Values sent between devices are 32-bit elements; how exact they have to be, the bound alone decides.
No kernel may reach another device: no remote copies, remote signals or barrier semaphores. Data moves between devices by JAX's collectives and lax.ppermute only.
A program may use at most 64 MiB of HBM per device.

v0:
```python
import math
import jax
import jax.numpy as jnp
from jax import lax
from jax.sharding import PartitionSpec as P

ITERS = 4
precise = lax.Precision.HIGHEST


def padded(block, sides, width):
    for axis, dim in sides:
        count = lax.axis_size(axis)
        forward = [(i, i + 1) for i in range(count - 1)]
        backward = [(target, source) for source, target in forward]
        low = lax.ppermute(
            lax.slice_in_dim(block, block.shape[dim] - width, None, axis=dim), axis, forward
        )
        high = lax.ppermute(lax.slice_in_dim(block, 0, width, axis=dim), axis, backward)
        block = jnp.concatenate([low, block, high], axis=dim)
    return block


def split_length(length):
    second = min(128, length)
    return (length // second, second)


def phase_table(height, breadth, modulus, orient):
    product = (
        lax.broadcasted_iota(jnp.int32, (height, breadth), 0)
        * lax.broadcasted_iota(jnp.int32, (height, breadth), 1)
        % modulus
    )
    angles = product.astype(jnp.float32) * (orient * 2.0 * math.pi / modulus)
    return (jnp.cos(angles), jnp.sin(angles))


def true_freq(index, factor, second):
    return index // second + factor * (index % second)


def forward_permuted(real_part, imag_part, orient):
    length = real_part.shape[-1]
    factor, second = split_length(length)
    leading = real_part.shape[:-1]
    inner_cos, inner_sin = phase_table(factor, factor, factor, orient)
    shaped = real_part.reshape(leading + (factor, second))
    section_real = jnp.einsum("kn,...na->...ka", inner_cos, shaped, precision=precise)
    section_imag = jnp.einsum("kn,...na->...ka", inner_sin, shaped, precision=precise)
    if imag_part is not None:
        shaped_imag = imag_part.reshape(leading + (factor, second))
        section_real = section_real - jnp.einsum(
            "kn,...na->...ka", inner_sin, shaped_imag, precision=precise
        )
        section_imag = section_imag + jnp.einsum(
            "kn,...na->...ka", inner_cos, shaped_imag, precision=precise
        )
    twist_cos, twist_sin = phase_table(factor, second, length, orient)
    turned_real = section_real * twist_cos - section_imag * twist_sin
    turned_imag = section_real * twist_sin + section_imag * twist_cos
    outer_cos, outer_sin = phase_table(second, second, second, orient)
    result_real = jnp.einsum(
        "ja,...ka->...kj", outer_cos, turned_real, precision=precise
    ) - jnp.einsum("ja,...ka->...kj", outer_sin, turned_imag, precision=precise)
    result_imag = jnp.einsum(
        "ja,...ka->...kj", outer_sin, turned_real, precision=precise
    ) + jnp.einsum("ja,...ka->...kj", outer_cos, turned_imag, precision=precise)
    return (result_real.reshape(leading + (length,)), result_imag.reshape(leading + (length,)))


def inverse_natural(real_part, imag_part, orient, keep, real_only=False):
    length = real_part.shape[-1]
    factor, second = split_length(length)
    leading = real_part.shape[:-1]
    shaped_real = real_part.reshape(leading + (factor, second))
    shaped_imag = imag_part.reshape(leading + (factor, second))
    inner_cos, inner_sin = phase_table(second, second, second, orient)
    section_real = jnp.einsum(
        "ak,...jk->...ja", inner_cos, shaped_real, precision=precise
    ) - jnp.einsum("ak,...jk->...ja", inner_sin, shaped_imag, precision=precise)
    section_imag = jnp.einsum(
        "ak,...jk->...ja", inner_sin, shaped_real, precision=precise
    ) + jnp.einsum("ak,...jk->...ja", inner_cos, shaped_imag, precision=precise)
    twist_cos, twist_sin = phase_table(factor, second, length, orient)
    turned_real = section_real * twist_cos - section_imag * twist_sin
    turned_imag = section_real * twist_sin + section_imag * twist_cos
    outer_cos, outer_sin = phase_table(keep // second, factor, factor, orient)
    result_real = jnp.einsum(
        "bj,...ja->...ba", outer_cos, turned_real, precision=precise
    ) - jnp.einsum("bj,...ja->...ba", outer_sin, turned_imag, precision=precise)
    result_real = result_real.reshape(leading + (keep,))
    if real_only:
        return (result_real, None)
    result_imag = jnp.einsum(
        "bj,...ja->...ba", outer_sin, turned_real, precision=precise
    ) + jnp.einsum("bj,...ja->...ba", outer_cos, turned_imag, precision=precise)
    return (result_real, result_imag.reshape(leading + (keep,)))


def amplitude(row_freq, col_freq, length, scale, wave):
    row_wave = jnp.minimum(row_freq, length - row_freq).astype(jnp.float32)
    col_wave = jnp.minimum(col_freq, length - col_freq).astype(jnp.float32)
    shape_term = 1.0 / (1.0 + (row_wave * row_wave + col_wave * col_wave) / (wave * wave))
    return scale * length / (wave * math.sqrt(math.pi)) * shape_term


def body(state, noise, step, field_scale, wave_scale, source, obs_cells, obs_values):
    parts = lax.axis_size("strip")
    position = lax.axis_index("strip")
    rows_here, length = state.shape
    half = length // 2
    factor, second = split_length(length)
    field_rows = source.shape[0]
    rate = step[0]
    sigma = field_scale[0]
    wave = wave_scale[0]
    mixed = jnp.sqrt(1.0 - rate * rate) * state + rate * noise
    row_freq = true_freq(lax.broadcasted_iota(jnp.int32, (1, length), 1), factor, second)
    width = length // parts
    freq_real, freq_imag = forward_permuted(mixed, None, -1.0)
    send_real = freq_real.reshape(rows_here, parts, width).transpose(1, 2, 0)
    send_imag = freq_imag.reshape(rows_here, parts, width).transpose(1, 2, 0)
    column_real, column_imag = (
        lax.all_to_all(send_real, "strip", split_axis=0, concat_axis=2, tiled=True),
        lax.all_to_all(send_imag, "strip", split_axis=0, concat_axis=2, tiled=True),
    )
    column_real = column_real.reshape(width, length)
    column_imag = column_imag.reshape(width, length)
    spec_real, spec_imag = forward_permuted(column_real, column_imag, -1.0)
    slot = position * width + lax.broadcasted_iota(jnp.int32, (width, 1), 0)
    col_freq = true_freq(slot, factor, second)
    scaled = amplitude(row_freq, col_freq, length, sigma, wave)
    field_real, field_imag = inverse_natural(scaled * spec_real, scaled * spec_imag, 1.0, half)
    back_real, back_imag = (
        lax.all_to_all(
            field_real.reshape(width, parts, field_rows),
            "strip",
            split_axis=1,
            concat_axis=0,
            tiled=True,
        ),
        lax.all_to_all(
            field_imag.reshape(width, parts, field_rows),
            "strip",
            split_axis=1,
            concat_axis=0,
            tiled=True,
        ),
    )
    lower_real = back_real.reshape(length, field_rows).T
    lower_imag = back_imag.reshape(length, field_rows).T
    log_perm = inverse_natural(lower_real, lower_imag, 1.0, half, True)[0] / (length * length)
    kappa = jnp.exp(log_perm)
    rimmed = padded(kappa, (("strip", 0),), 1)
    sided = jnp.pad(kappa, ((0, 0), (1, 1)))
    north = 0.5 * (kappa + rimmed[:-2])
    south = 0.5 * (kappa + rimmed[2:])
    west = 0.5 * (kappa + sided[:, :-2])
    east = 0.5 * (kappa + sided[:, 2:])
    diagonal = north + south + west + east
    pressure = jnp.zeros_like(source)
    residual = source
    direction = jnp.zeros_like(source)
    along = jnp.zeros_like(source)
    gamma_prior = jnp.float32(1.0)
    alpha_prior = jnp.float32(1.0)
    for iteration in range(ITERS):
        precond = residual / diagonal
        beside_all = padded(precond, (("strip", 0),), 1)
        beside = jnp.pad(precond, ((0, 0), (1, 1)))
        image = (
            diagonal * precond
            - north * beside_all[:-2]
            - south * beside_all[2:]
            - west * beside[:, :-2]
            - east * beside[:, 2:]
        )
        gamma, delta = lax.psum((jnp.sum(residual * precond), jnp.sum(precond * image)), "strip")
        if iteration == 0:
            alpha = gamma / delta
            direction = precond
            along = image
        else:
            ratio = gamma / gamma_prior
            alpha = gamma / (delta - ratio * gamma / alpha_prior)
            direction = precond + ratio * direction
            along = image + ratio * along
        pressure = pressure + alpha * direction
        residual = residual - alpha * along
        gamma_prior = gamma
        alpha_prior = alpha
    columns = pressure.shape[1]
    cell_row = obs_cells // columns
    cell_col = obs_cells % columns
    local_row = cell_row - position * field_rows
    inside = (local_row >= 0) & (local_row < field_rows)
    picked = pressure[jnp.clip(local_row, 0, field_rows - 1), cell_col]
    differ = jnp.where(inside, picked - obs_values, 0.0)
    total = lax.psum(jnp.sum(differ * differ), "strip")
    loglik = -(2.0 / obs_cells.shape[0]) * total
    return (log_perm, pressure, loglik)


def solution(mesh):
    placed = (P("strip", None), P("strip", None), P(), P(), P(), P("strip", None), P(), P())
    return jax.shard_map(
        body,
        mesh=mesh,
        in_specs=placed,
        out_specs=(P("strip", None), P("strip", None), P()),
        check_vma=False,
    )
```

profile of v0, /device:TPU:0, one launch (start us, length us, event | category | flops | bytes accessed | tf_op | source)
XLA Modules:
  0.0 528.5 jit_solution(12919456128651827685)
XLA Ops:
  1.4 2.5 add_bitcast_fusion.1
  4.3 2.0 fusion.176
  6.2 2.4 fusion.2
  8.6 3.6 fusion.22
  12.2 5.2 subtract_bitcast_fusion
  17.5 7.5 %all-to-all-start = ((f32[32,128,128]{1,2,0:T(8,128)}), f32[32,128,128]{1,2,0:T(8,128)}, u32[]{:S(2)}, u32[]{:S(2)}) async-start(f32[32,128,128]{1,2,0:T(8,128)} %subtract_bitcast_fusion), calls=%async_computation | async-start | bytes 4194304 | tf_op jit(solution)/shard_map/all_to_all | solution.py:125
  24.9 5.1 fusion.20
  30.1 4.9 add_bitcast_fusion
  35.0 38.6 %all-to-all-done = f32[32,128,128]{1,2,0:T(8,128)} async-done(((f32[32,128,128]{1,2,0:T(8,128)}), f32[32,128,128]{1,2,0:T(8,128)}, u32[]{:S(2)}, u32[]{:S(2)}) %all-to-all-start) | async-done | bytes 2097184 | tf_op jit(solution)/shard_map/all_to_all | solution.py:125
  73.7 4.2 all-to-all-start.1
  79.4 2.4 copy.29
  81.8 3.3 fusion.174
  85.1 3.3 fusion.168
  88.4 38.2 %all-to-all-done.1 = f32[32,128,128]{1,2,0:T(8,128)} async-done(((f32[32,128,128]{1,2,0:T(8,128)}), f32[32,128,128]{1,2,0:T(8,128)}, u32[]{:S(2)}, u32[]{:S(2)}) %all-to-all-start.1) | async-done | bytes 2097184 | tf_op jit(solution)/shard_map/all_to_all | solution.py:126
  126.6 2.5 copy.32
  129.2 3.8 convolution_subtract_fusion
  133.0 2.5 fusion
  135.5 3.6 fusion.12
  139.2 3.6 fusion.14
  142.7 4.2 subtract_multiply_fusion
  147.0 2.1 fusion.114
  149.1 2.1 fusion.107
  151.3 3.9 add_multiply_fusion
  155.2 2.3 convolution_subtract_fusion.1
  157.5 2.4 multiply_subtract_fusion
  161.3 2.4 fusion.6
  163.7 2.4 fusion.39
  167.5 4.1 all-to-all-start.2
  171.6 3.9 fusion.4
  175.6 3.4 fusion.45
  179.0 2.6 copy.45
  181.6 16.3 %all-to-all-done.2 = f32[128,32,64]{0,2,1:T(8,128)S(1)} async-done(((f32[128,32,64]{0,2,1:T(8,128)}), f32[128,32,64]{0,2,1:T(8,128)S(1)}, u32[]{:S(2)}, u32[]{:S(2)}) %all-to-all-start.2) | async-done | bytes 1048608 | tf_op jit(solution)/shard_map/all_to_all | solution.py:136
  197.8 4.0 all-to-all-start.3
  205.7 22.3 %all-to-all-done.3 = f32[128,32,64]{0,2,1:T(8,128)} async-done(((f32[128,32,64]{0,2,1:T(8,128)}), f32[128,32,64]{0,2,1:T(8,128)}, u32[]{:S(2)}, u32[]{:S(2)}) %all-to-all-start.3) | async-done | bytes 1048608 | tf_op jit(solution)/shard_map/all_to_all | solution.py:143
  238.4 3.5 collective-permute-done.1
  242.3 4.3 collective-permute-start.2
  250.8 43.0 %all-reduce.8 = (f32[]{:T(128)}, f32[]{:T(128)}) all-reduce(f32[]{:T(128)} %get-tuple-element.10, f32[]{:T(128)} %get-tuple-element.9), channel_id=1, replica_groups=mesh['strip'=32] {'strip'}, use_global_device_ids=true, to_apply=%region_1.2 | all-reduce | flops 2 | bytes 16 | tf_op jit(solution)/shard_map/psum | solution.py:179
  298.9 4.3 collective-permute-done.5
  303.1 2.0 multiply_reduce_fusion.3
  305.1 41.9 %all-reduce.7 = (f32[]{:T(128)}, f32[]{:T(128)}) all-reduce(f32[]{:T(128)} %get-tuple-element.8, f32[]{:T(128)} %get-tuple-element.7), channel_id=1, replica_groups=mesh['strip'=32] {'strip'}, use_global_device_ids=true, to_apply=%region_5.6 | all-reduce | flops 2 | bytes 16 | tf_op jit(solution)/shard_map/psum | solution.py:179
  351.6 2.1 fusion.343
  357.1 4.3 collective-permute-done.7
  361.4 4.3 multiply_reduce_fusion.1
  365.7 41.8 %all-reduce.6 = (f32[]{:T(128)}, f32[]{:T(128)}) all-reduce(f32[]{:T(128)} %get-tuple-element.6, f32[]{:T(128)} %get-tuple-element.5), channel_id=1, replica_groups=mesh['strip'=32] {'strip'}, use_global_device_ids=true, to_apply=%region_9.10 | all-reduce | flops 2 | bytes 16 | tf_op jit(solution)/shard_map/psum | solution.py:179
  415.9 4.2 collective-permute-done.9
  421.2 41.9 %all-reduce.5 = (f32[]{:T(128)}, f32[]{:T(128)}) all-reduce(f32[]{:T(128)} %get-tuple-element.4, f32[]{:T(128)} %get-tuple-element.3), channel_id=1, replica_groups=mesh['strip'=32] {'strip'}, use_global_device_ids=true, to_apply=%region_13.14 | all-reduce | flops 2 | bytes 16 | tf_op jit(solution)/shard_map/psum | solution.py:179
  468.8 16.6 %gather_fusion = f32[2048]{0:T(1024)S(1)} fusion(f32[64,2048]{1,0:T(8,128)S(1)} %multiply_add_fusion.1, s32[2048]{0:T(1024)S(1)} %fusion.195), kind=kCustom, calls=%fused_computation | custom fusion | bytes 32768 | tf_op jit(solution)/shard_map/gather | solution.py:198
  486.1 40.2 %psum.71 = f32[]{:T(128)} all-reduce(f32[]{:T(128)} %multiply_reduce_fusion.7), channel_id=1, replica_groups=mesh['strip'=32] {'strip'}, use_global_device_ids=true, to_apply=%region_17.18 | all-reduce | flops 1 | bytes 8 | tf_op jit(solution)/shard_map/psum | solution.py:200
  (69 shorter events, 36.7 us)
Async XLA Ops:
  8.6 3.6 copy-start.2
  17.5 56.2 %all-to-all-start = ((f32[32,128,128]{1,2,0:T(8,128)}), f32[32,128,128]{1,2,0:T(8,128)}, u32[]{:S(2)}, u32[]{:S(2)}) async-start(f32[32,128,128]{1,2,0:T(8,128)} %subtract_bitcast_fusion), calls=%async_computation | async-start | bytes 4194304 | tf_op jit(solution)/shard_map/all_to_all | solution.py:125
  73.7 52.9 %all-to-all-start.1 = ((f32[32,128,128]{1,2,0:T(8,128)}), f32[32,128,128]{1,2,0:T(8,128)}, u32[]{:S(2)}, u32[]{:S(2)}) async-start(f32[32,128,128]{1,2,0:T(8,128)} %add_bitcast_fusion), calls=%async_computation.1 | async-start | bytes 4194304 | tf_op jit(solution)/shard_map/all_to_all | solution.py:126
  129.2 3.8 copy-start.3
  159.9 1.3 copy-start.1
  167.5 30.3 %all-to-all-start.2 = ((f32[128,32,64]{0,2,1:T(8,128)}), f32[128,32,64]{0,2,1:T(8,128)S(1)}, u32[]{:S(2)}, u32[]{:S(2)}) async-start(f32[128,32,64]{0,2,1:T(8,128)} %bitcast.183), calls=%async_computation.2 | async-start | bytes 2097152 | tf_op jit(solution)/shard_map/all_to_all | solution.py:136
  197.8 30.1 %all-to-all-start.3 = ((f32[128,32,64]{0,2,1:T(8,128)}), f32[128,32,64]{0,2,1:T(8,128)}, u32[]{:S(2)}, u32[]{:S(2)}) async-start(f32[128,32,64]{0,2,1:T(8,128)} %bitcast.33), calls=%async_computation.3 | async-start | bytes 2097152 | tf_op jit(solution)/shard_map/all_to_all | solution.py:143
  233.9 7.9 %copy-start.7 = (f32[64,2048]{1,0:T(8,128)S(1)}, f32[64,2048]{1,0:T(8,128)}, u32[]{:S(2)}) copy-start(f32[64,2048]{1,0:T(8,128)} %param.13) | copy-start | bytes 1572868
  235.8 2.6 collective-permute-start
  237.1 4.8 collective-permute-start.1
  242.3 5.6 %collective-permute-start.2 = (f32[1,2048]{1,0:T(1,128)S(1)}, f32[1,2048]{1,0:T(1,128)S(1)}, u32[]{:S(2)}, u32[]{:S(2)}) collective-permute-start(f32[1,2048]{1,0:T(1,128)S(1)} %get-tuple-element.46), channel_id=1, source_target_pairs={{0,1},{1,2},{2,3},{3,4},{4,5},{5,6},{6,7},{7,8},{8,9},{9,10},{10,1... | collective-permute-start | bytes 24584 | tf_op jit(solution)/shard_map/ppermute | solution.py:16
  246.6 3.1 collective-permute-start.3
  296.2 6.9 %copy-start.4 = (f32[64,2048]{1,0:T(8,128)}, f32[64,2048]{1,0:T(8,128)S(1)}, u32[]{:S(2)}) copy-start(f32[64,2048]{1,0:T(8,128)S(1)} %get-tuple-element.25) | copy-start | bytes 1572868
  296.2 8.9 %copy-start.8 = (f32[64,2048]{1,0:T(8,128)}, f32[64,2048]{1,0:T(8,128)S(1)}, u32[]{:S(2)}) copy-start(f32[64,2048]{1,0:T(8,128)S(1)} %get-tuple-element.26) | copy-start | bytes 1572868
  296.2 2.6 collective-permute-start.4
  297.5 5.6 %collective-permute-start.5 = (f32[1,2048]{1,0:T(1,128)S(1)}, f32[1,2048]{1,0:T(1,128)S(1)}, u32[]{:S(2)}, u32[]{:S(2)}) collective-permute-start(f32[1,2048]{1,0:T(1,128)S(1)} %get-tuple-element.45), channel_id=1, source_target_pairs={{1,0},{2,1},{3,2},{4,3},{5,4},{6,5},{7,6},{8,7},{9,8},{10,9},{11,1... | collective-permute-start | bytes 24584 | tf_op jit(solution)/shard_map/ppermute | solution.py:19
  353.7 0.8 copy-start.5
  354.5 2.6 collective-permute-start.6
  355.8 5.6 %collective-permute-start.7 = (f32[1,2048]{1,0:T(1,128)S(1)}, f32[1,2048]{1,0:T(1,128)S(1)}, u32[]{:S(2)}, u32[]{:S(2)}) collective-permute-start(f32[1,2048]{1,0:T(1,128)S(1)} %get-tuple-element.43), channel_id=1, source_target_pairs={{1,0},{2,1},{3,2},{4,3},{5,4},{6,5},{7,6},{8,7},{9,8},{10,9},{11,1... | collective-permute-start | bytes 24584 | tf_op jit(solution)/shard_map/ppermute | solution.py:19
  365.7 50.1 %copy-start.9 = (s32[2048]{0:T(1024)S(1)}, s32[2048]{0:T(1024)}, u32[]{:S(2)}) copy-start(s32[2048]{0:T(1024)} %param.14) | copy-start | bytes 24580
  413.2 8.0 %copy-start.6 = (f32[64,2048]{1,0:T(8,128)}, f32[64,2048]{1,0:T(8,128)S(1)}, u32[]{:S(2)}) copy-start(f32[64,2048]{1,0:T(8,128)S(1)} %get-tuple-element.19) | copy-start | bytes 1572868
  413.2 2.6 collective-permute-start.8
  414.5 5.6 %collective-permute-start.9 = (f32[1,2048]{1,0:T(1,128)S(1)}, f32[1,2048]{1,0:T(1,128)S(1)}, u32[]{:S(2)}, u32[]{:S(2)}) collective-permute-start(f32[1,2048]{1,0:T(1,128)S(1)} %get-tuple-element.41), channel_id=1, source_target_pairs={{1,0},{2,1},{3,2},{4,3},{5,4},{6,5},{7,6},{8,7},{9,8},{10,9},{11,1... | collective-permute-start | bytes 24584 | tf_op jit(solution)/shard_map/ppermute | solution.py:19
  468.7 16.7 %copy-start = (f32[64,2048]{1,0:T(8,128)}, f32[64,2048]{1,0:T(8,128)S(1)}, u32[]{:S(2)}) copy-start(f32[64,2048]{1,0:T(8,128)S(1)} %multiply_add_fusion.1) | copy-start | bytes 1572868
  468.8 16.7 %copy-start.10 = (f32[2048]{0:T(1024)S(1)}, f32[2048]{0:T(1024)}, u32[]{:S(2)}) copy-start(f32[2048]{0:T(1024)} %param.15) | copy-start | bytes 24580
where the time goes:
time: 539 us; the launch traced here: 528 us
  blocking collectives  209 us (39%)
  waiting for transfers between devices  133 us (25%)
  matrix products  79.3 us (15%)
  starting transfers between devices  35.6 us (7%)
  local copies, waits for them, and re-layouts  33.2 us (6%)
  between operations  19.5 us (4%)
  other arithmetic  18.7 us (3%)
    psum x4, blocking collectives, body(): lax.psum((jnp.sum(residual * precond), jnp.sum(precond * image)), 'strip')  169 us
    psum x1, blocking collectives, body(): total = lax.psum(jnp.sum(differ * differ), 'strip')  40.2 us
    all_to_all x1, waiting for transfers between devices, body(): lax.all_to_all(send_real, 'strip', split_axis=0, concat_axis=2, tiled=True)  38.6 us
    all_to_all x1, waiting for transfers between devices, body(): lax.all_to_all(send_imag, 'strip', split_axis=0, concat_axis=2, tiled=True)  38.2 us
    all_to_all x1, waiting for transfers between devices, body(): lax.all_to_all(field_imag.reshape(width, parts, field_rows), 'strip', spl...  22.3 us
    ppermute x5, waiting for transfers between devices, padded(): lax.ppermute(lax.slice_in_dim(block, 0, width, axis=dim), axis, backward)  18 us
    gather x1, local copies, waits for them, and re-layouts, body(): picked = pressure[jnp.clip(local_row, 0, field_rows - 1), cell_col]  16.6 us
    all_to_all x1, waiting for transfers between devices, body(): lax.all_to_all(field_real.reshape(width, parts, field_rows), 'strip', spl...  16.3 us
  transfers between devices with their start and end apart: 14, of which 9 were waited for; matrix products, arithmetic and copies ran while one was open for 6% of the time, Pallas kernels for 0%

commit v1 on v0

--- a/solution.py
+++ b/solution.py
@@ -6,6 +6,12 @@
 
 ITERS = 4
 precise = lax.Precision.HIGHEST
+
+
+def trade_parts(block, name, split, join):
+    cells = jnp.split(block, lax.axis_size(name), axis=split)
+    incoming = lax.all_to_all(jnp.stack(cells), name, 0, 0)
+    return jnp.concatenate(incoming, axis=join)
 
 
 def padded(block, sides, width):
@@ -140,13 +146,7 @@
             concat_axis=0,
             tiled=True,
         ),
-        lax.all_to_all(
-            field_imag.reshape(width, parts, field_rows),
-            "strip",
-            split_axis=1,
-            concat_axis=0,
-            tiled=True,
-        ),
+        trade_parts(field_imag.reshape(width, parts, field_rows), "strip", 1, 0),
     )
     lower_real = back_real.reshape(length, field_rows).T
     lower_imag = back_imag.reshape(length, field_rows).T

time: 539 us -> 560 us (1.039)
  local copies, waits for them, and re-layouts: 33.2 us -> 50.8 us
    unnamed x27 -> x58, local copies, waits for them, and re-layouts: 4.11 us -> 21.8 us
  transfers between devices with their start and end apart: 14 -> 14, of which waited for: 9 -> 9; matrix products, arithmetic and copies ran while one was open for 6% -> 5% of each run, Pallas kernels for 0% -> 0%
where the time goes in v1:
time: 560 us; the launch traced here: 550 us
  blocking collectives  209 us (37%)
  waiting for transfers between devices  137 us (24%)
  matrix products  79.6 us (14%)
  local copies, waits for them, and re-layouts  50.8 us (9%)
  starting transfers between devices  35.3 us (6%)
  between operations  19.2 us (3%)
  other arithmetic  18.7 us (3%)
    psum x4, blocking collectives, body(): lax.psum((jnp.sum(residual * precond), jnp.sum(precond * image)), 'strip')  169 us
    psum x1, blocking collectives, body(): total = lax.psum(jnp.sum(differ * differ), 'strip')  40.2 us
    all_to_all x1, waiting for transfers between devices, body(): lax.all_to_all(send_real, 'strip', split_axis=0, concat_axis=2, tiled=True)  38.6 us
    all_to_all x1, waiting for transfers between devices, body(): lax.all_to_all(send_imag, 'strip', split_axis=0, concat_axis=2, tiled=True)  38.2 us
    all_to_all x1, waiting for transfers between devices, trade_parts(): incoming = lax.all_to_all(jnp.stack(cells), name, 0, 0)  22.3 us
    unnamed x58, local copies, waits for them, and re-layouts  21.8 us
    all_to_all x1, waiting for transfers between devices, body(): lax.all_to_all(field_real.reshape(width, parts, field_rows), 'strip', spl...  20.1 us
    ppermute x5, waiting for transfers between devices, padded(): lax.ppermute(lax.slice_in_dim(block, 0, width, axis=dim), axis, backward)  18 us
  transfers between devices with their start and end apart: 14, of which 9 were waited for; matrix products, arithmetic and copies ran while one was open for 5% of the time, Pallas kernels for 0%

profile of v1, /device:TPU:0, one launch (start us, length us, event | category | flops | bytes accessed | tf_op | source)
XLA Modules:
  0.0 549.5 jit_solution(11513130941605076728)
XLA Ops:
  1.4 2.5 add_bitcast_fusion.1
  4.3 2.0 fusion.176
  6.2 2.4 fusion.2
  8.6 3.6 fusion.22
  12.2 5.1 subtract_bitcast_fusion
  17.3 7.5 %all-to-all-start = ((f32[32,128,128]{1,2,0:T(8,128)}), f32[32,128,128]{1,2,0:T(8,128)}, u32[]{:S(2)}, u32[]{:S(2)}) async-start(f32[32,128,128]{1,2,0:T(8,128)} %subtract_bitcast_fusion), calls=%async_computation | async-start | bytes 4194304 | tf_op jit(solution)/shard_map/all_to_all | solution.py:131
  24.8 5.1 fusion.20
  29.9 4.9 add_bitcast_fusion
  34.8 38.6 %all-to-all-done = f32[32,128,128]{1,2,0:T(8,128)} async-done(((f32[32,128,128]{1,2,0:T(8,128)}), f32[32,128,128]{1,2,0:T(8,128)}, u32[]{:S(2)}, u32[]{:S(2)}) %all-to-all-start) | async-done | bytes 2097184 | tf_op jit(solution)/shard_map/all_to_all | solution.py:131
  73.5 4.2 all-to-all-start.1
  79.2 2.4 copy.80
  81.6 3.3 fusion.174
  84.9 3.3 fusion.168
  88.2 38.2 %all-to-all-done.1 = f32[32,128,128]{1,2,0:T(8,128)} async-done(((f32[32,128,128]{1,2,0:T(8,128)}), f32[32,128,128]{1,2,0:T(8,128)}, u32[]{:S(2)}, u32[]{:S(2)}) %all-to-all-start.1) | async-done | bytes 2097184 | tf_op jit(solution)/shard_map/all_to_all | solution.py:132
  126.4 2.8 copy.83
  129.2 3.8 convolution_subtract_fusion
  133.1 2.5 fusion
  135.6 3.5 fusion.12
  139.2 3.6 fusion.14
  142.8 4.0 subtract_multiply_fusion
  146.8 2.1 fusion.114
  148.9 2.1 fusion.107
  151.1 3.9 add_multiply_fusion
  155.0 2.5 convolution_subtract_fusion.1
  157.5 2.4 multiply_subtract_fusion
  159.9 2.4 fusion.4
  162.3 3.4 fusion.6
  165.7 3.4 fusion.45
  184.4 3.4 fusion.39
  187.9 2.6 copy.92
  190.4 4.1 all-to-all-start.2
  200.6 20.1 %all-to-all-done.2 = f32[128,32,64]{0,2,1:T(8,128)S(1)} async-done(((f32[128,32,64]{0,2,1:T(8,128)}), f32[128,32,64]{0,2,1:T(8,128)S(1)}, u32[]{:S(2)}, u32[]{:S(2)}) %all-to-all-start.2) | async-done | bytes 1048608 | tf_op jit(solution)/shard_map/all_to_all | solution.py:142
  220.7 3.6 all-to-all-start.3
  228.2 22.3 %all-to-all-done.3 = f32[32,128,1,64]{1,3,2,0:T(8,128)S(1)} async-done(((f32[32,128,1,64]{1,3,2,0:T(8,128)}), f32[32,128,1,64]{1,3,2,0:T(8,128)S(1)}, u32[]{:S(2)}, u32[]{:S(2)}) %all-to-all-start.3) | async-done | bytes 1048608 | tf_op jit(solution)/shard_map/all_to_all | solution.py:13
  259.7 3.5 collective-permute-done.1
  263.6 4.3 collective-permute-start.2
  272.1 43.0 %all-reduce.8 = (f32[]{:T(128)}, f32[]{:T(128)}) all-reduce(f32[]{:T(128)} %get-tuple-element.10, f32[]{:T(128)} %get-tuple-element.9), channel_id=1, replica_groups=mesh['strip'=32] {'strip'}, use_global_device_ids=true, to_apply=%region_1.2 | all-reduce | flops 2 | bytes 16 | tf_op jit(solution)/shard_map/psum | solution.py:179
  320.2 4.3 collective-permute-done.5
  324.4 2.0 multiply_reduce_fusion.3
  326.4 41.8 %all-reduce.7 = (f32[]{:T(128)}, f32[]{:T(128)}) all-reduce(f32[]{:T(128)} %get-tuple-element.8, f32[]{:T(128)} %get-tuple-element.7), channel_id=1, replica_groups=mesh['strip'=32] {'strip'}, use_global_device_ids=true, to_apply=%region_5.6 | all-reduce | flops 2 | bytes 16 | tf_op jit(solution)/shard_map/psum | solution.py:179
  372.9 2.1 fusion.343
  378.4 4.3 collective-permute-done.7
  382.7 4.3 multiply_reduce_fusion.1
  387.0 41.8 %all-reduce.6 = (f32[]{:T(128)}, f32[]{:T(128)}) all-reduce(f32[]{:T(128)} %get-tuple-element.6, f32[]{:T(128)} %get-tuple-element.5), channel_id=1, replica_groups=mesh['strip'=32] {'strip'}, use_global_device_ids=true, to_apply=%region_9.10 | all-reduce | flops 2 | bytes 16 | tf_op jit(solution)/shard_map/psum | solution.py:179
  437.2 4.2 collective-permute-done.9
  442.5 41.9 %all-reduce.5 = (f32[]{:T(128)}, f32[]{:T(128)}) all-reduce(f32[]{:T(128)} %get-tuple-element.4, f32[]{:T(128)} %get-tuple-element.3), channel_id=1, replica_groups=mesh['strip'=32] {'strip'}, use_global_device_ids=true, to_apply=%region_13.14 | all-reduce | flops 2 | bytes 16 | tf_op jit(solution)/shard_map/psum | solution.py:179
  490.1 16.6 %gather_fusion = f32[2048]{0:T(1024)S(1)} fusion(f32[64,2048]{1,0:T(8,128)S(1)} %multiply_add_fusion.1, s32[2048]{0:T(1024)S(1)} %fusion.195), kind=kCustom, calls=%fused_computation | custom fusion | bytes 32768 | tf_op jit(solution)/shard_map/gather | solution.py:198
  507.4 40.2 %psum.71 = f32[]{:T(128)} all-reduce(f32[]{:T(128)} %multiply_reduce_fusion.7), channel_id=1, replica_groups=mesh['strip'=32] {'strip'}, use_global_device_ids=true, to_apply=%region_17.18 | all-reduce | flops 1 | bytes 8 | tf_op jit(solution)/shard_map/psum | solution.py:200
  (101 shorter events, 54.1 us)
Async XLA Ops:
  8.6 3.6 copy-start.1
  17.3 56.2 %all-to-all-start = ((f32[32,128,128]{1,2,0:T(8,128)}), f32[32,128,128]{1,2,0:T(8,128)}, u32[]{:S(2)}, u32[]{:S(2)}) async-start(f32[32,128,128]{1,2,0:T(8,128)} %subtract_bitcast_fusion), calls=%async_computation | async-start | bytes 4194304 | tf_op jit(solution)/shard_map/all_to_all | solution.py:131
  73.5 52.9 %all-to-all-start.1 = ((f32[32,128,128]{1,2,0:T(8,128)}), f32[32,128,128]{1,2,0:T(8,128)}, u32[]{:S(2)}, u32[]{:S(2)}) async-start(f32[32,128,128]{1,2,0:T(8,128)} %add_bitcast_fusion), calls=%async_computation.1 | async-start | bytes 4194304 | tf_op jit(solution)/shard_map/all_to_all | solution.py:132
  129.2 3.8 copy-start.2
  170.9 13.5 %copy-start.8 = (f32[128,128,16]{1,2,0:T(8,128)S(1)}, f32[128,128,16]{1,2,0:T(8,128)}, u32[]{:S(2)}) copy-start(f32[128,128,16]{1,2,0:T(8,128)} %fusion.6) | copy-start | bytes 3145732
  190.4 30.3 %all-to-all-start.2 = ((f32[128,32,64]{0,2,1:T(8,128)}), f32[128,32,64]{0,2,1:T(8,128)S(1)}, u32[]{:S(2)}, u32[]{:S(2)}) async-start(f32[128,32,64]{0,2,1:T(8,128)} %bitcast.28), calls=%async_computation.2 | async-start | bytes 2097152 | tf_op jit(solution)/shard_map/all_to_all | solution.py:142
  220.7 29.8 %all-to-all-start.3 = ((f32[32,128,1,64]{1,3,2,0:T(8,128)}), f32[32,128,1,64]{1,3,2,0:T(8,128)S(1)}, u32[]{:S(2)}, u32[]{:S(2)}) async-start(f32[32,128,1,64]{1,3,2,0:T(8,128)} %constant_dynamic-update-slice_fusion), calls=%async_computation.3 | async-start | bytes 2097152 | tf_op jit(solution)/shard_map/all_to_all | solution.py:13
  255.3 7.9 %copy-start.6 = (f32[64,2048]{1,0:T(8,128)S(1)}, f32[64,2048]{1,0:T(8,128)}, u32[]{:S(2)}) copy-start(f32[64,2048]{1,0:T(8,128)} %param.13) | copy-start | bytes 1572868
  257.1 2.6 collective-permute-start
  258.4 4.8 collective-permute-start.1
  263.6 5.6 %collective-permute-start.2 = (f32[1,2048]{1,0:T(1,128)S(1)}, f32[1,2048]{1,0:T(1,128)S(1)}, u32[]{:S(2)}, u32[]{:S(2)}) collective-permute-start(f32[1,2048]{1,0:T(1,128)S(1)} %get-tuple-element.46), channel_id=1, source_target_pairs={{0,1},{1,2},{2,3},{3,4},{4,5},{5,6},{6,7},{7,8},{8,9},{9,10},{10,1... | collective-permute-start | bytes 24584 | tf_op jit(solution)/shard_map/ppermute | solution.py:22
  268.0 3.1 collective-permute-start.3
  317.5 6.9 %copy-start.3 = (f32[64,2048]{1,0:T(8,128)}, f32[64,2048]{1,0:T(8,128)S(1)}, u32[]{:S(2)}) copy-start(f32[64,2048]{1,0:T(8,128)S(1)} %get-tuple-element.25) | copy-start | bytes 1572868
  317.5 8.9 %copy-start.7 = (f32[64,2048]{1,0:T(8,128)}, f32[64,2048]{1,0:T(8,128)S(1)}, u32[]{:S(2)}) copy-start(f32[64,2048]{1,0:T(8,128)S(1)} %get-tuple-element.26) | copy-start | bytes 1572868
  317.6 2.6 collective-permute-start.4
  318.9 5.6 %collective-permute-start.5 = (f32[1,2048]{1,0:T(1,128)S(1)}, f32[1,2048]{1,0:T(1,128)S(1)}, u32[]{:S(2)}, u32[]{:S(2)}) collective-permute-start(f32[1,2048]{1,0:T(1,128)S(1)} %get-tuple-element.45), channel_id=1, source_target_pairs={{1,0},{2,1},{3,2},{4,3},{5,4},{6,5},{7,6},{8,7},{9,8},{10,9},{11,1... | collective-permute-start | bytes 24584 | tf_op jit(solution)/shard_map/ppermute | solution.py:25
  375.0 0.8 copy-start.4
  375.8 2.6 collective-permute-start.6
  377.1 5.6 %collective-permute-start.7 = (f32[1,2048]{1,0:T(1,128)S(1)}, f32[1,2048]{1,0:T(1,128)S(1)}, u32[]{:S(2)}, u32[]{:S(2)}) collective-permute-start(f32[1,2048]{1,0:T(1,128)S(1)} %get-tuple-element.43), channel_id=1, source_target_pairs={{1,0},{2,1},{3,2},{4,3},{5,4},{6,5},{7,6},{8,7},{9,8},{10,9},{11,1... | collective-permute-start | bytes 24584 | tf_op jit(solution)/shard_map/ppermute | solution.py:25
  387.0 50.1 %copy-start.9 = (s32[2048]{0:T(1024)S(1)}, s32[2048]{0:T(1024)}, u32[]{:S(2)}) copy-start(s32[2048]{0:T(1024)} %param.14) | copy-start | bytes 24580
  434.5 8.0 %copy-start.5 = (f32[64,2048]{1,0:T(8,128)}, f32[64,2048]{1,0:T(8,128)S(1)}, u32[]{:S(2)}) copy-start(f32[64,2048]{1,0:T(8,128)S(1)} %get-tuple-element.19) | copy-start | bytes 1572868
  434.5 2.6 collective-permute-start.8
  435.8 5.6 %collective-permute-start.9 = (f32[1,2048]{1,0:T(1,128)S(1)}, f32[1,2048]{1,0:T(1,128)S(1)}, u32[]{:S(2)}, u32[]{:S(2)}) collective-permute-start(f32[1,2048]{1,0:T(1,128)S(1)} %get-tuple-element.41), channel_id=1, source_target_pairs={{1,0},{2,1},{3,2},{4,3},{5,4},{6,5},{7,6},{8,7},{9,8},{10,9},{11,1... | collective-permute-start | bytes 24584 | tf_op jit(solution)/shard_map/ppermute | solution.py:25
  490.0 16.7 %copy-start = (f32[64,2048]{1,0:T(8,128)}, f32[64,2048]{1,0:T(8,128)S(1)}, u32[]{:S(2)}) copy-start(f32[64,2048]{1,0:T(8,128)S(1)} %multiply_add_fusion.1) | copy-start | bytes 1572868
  490.1 16.7 %copy-start.10 = (f32[2048]{0:T(1024)S(1)}, f32[2048]{0:T(1024)}, u32[]{:S(2)}) copy-start(f32[2048]{0:T(1024)} %param.15) | copy-start | bytes 24580
